TPU v7x, 16 devices: a whole 2x2x2 slice. The times are simulated.
16 devices in a mesh: tp: 2 (over z), dp: 8 (over y, x, core).
Axes of the slice: x: 2, y: 2, z: 2, core: 2. Of those that a mesh axis runs over, the one named last changes fastest.
Arguments:
- w_in: float32 [1, 1408, 10368], P(None, None, 'tp')
- w_out: float32 [1, 7552, 1408], P(None, 'tp')
- g_in: float32 [8, 1, 1408, 10368], P('dp', None, None, 'tp')
- g_out: float32 [8, 1, 7552, 1408], P('dp', None, 'tp')
- m_in: bfloat16 [1, 1408, 10368], P(None, 'dp', 'tp')
- m_out: bfloat16 [1, 7552, 1408], P(None, 'tp', 'dp')
- r_in: float32 [1, 1408], P(None, 'dp')
- c_in: float32 [1, 10368], P(None, 'tp')
- r_out: float32 [1, 7552], P(None, 'tp')
- c_out: float32 [1, 1408], P(None, 'dp')
- learn_rate: float32 [], replicated
- weight_decay: float32 [], replicated
- beta_two: float32 [], replicated
Outputs:
- output 1: float32 [1, 1408, 10368], P(None, None, 'tp')
- output 2: float32 [1, 7552, 1408], P(None, 'tp')
- output 3: bfloat16 [1, 1408, 10368], P(None, 'dp', 'tp')
- output 4: bfloat16 [1, 7552, 1408], P(None, 'tp', 'dp')
- output 5: float32 [1, 1408], P(None, 'dp')
- output 6: float32 [1, 10368], P(None, 'tp')
- output 7: float32 [1, 7552], P(None, 'tp')
- output 8: float32 [1, 1408], P(None, 'dp')
All inputs are finite; a program needn't handle non-finite values.
Results may differ from a plain program's by a relative error of at most 0.00125668.
Values sent between devices are 32-bit elements.
A program may use at most 1 GiB of HBM per device.

v0:
```python
import jax
import jax.numpy as jnp
from jax import lax
from jax.experimental import pallas as pl
from jax.experimental.pallas import tpu as pltpu
from jax.sharding import PartitionSpec as P


F32 = jnp.float32
LANES = 128
SUB = 8
DP = 8
EVERY = 16
ALL_VMEM = 67043328
BESIDE_HOLD = 45500000
YES, NO = True, False
BF16 = jnp.bfloat16
MESH = pl.DeviceIdType.MESH
NCH = 8
WINDOW = 384
ORDER = (0, 4, 1, 5, 2, 6, 3, 7)


def chunk_rows(rows, small_last):
    tiles = rows // SUB
    out, start = [], 0
    for part in ((tiles + 1) // 2, tiles // 2):
        sizes = [part // 10, part // 2 - part // 10, part // 4 + 1] if small_last else [part // 20, part * 9 // 40, part * 3 // 8]
        sizes.append(part - sum(sizes))
        for n in sizes[::-1] if small_last and out else sizes:
            out.append((SUB * start, SUB * n))
            start += n
    return out


def lane_chunks(total):
    width = SUB * LANES
    out = [(s, width) for s in range(0, total - width, width)]
    last = len(out) * width
    if total - last < width // 4:
        s, n = out.pop()
        return out + [(s, n + total - last)]
    return out + [(last, total - last)]


class Mat:
    def __init__(self, kloc, width, tp, row_is_r):
        self.k, self.width, self.sh = kloc, width, width // DP
        self.r = kloc // DP
        self.ktot = kloc * tp
        self.row_is_r = row_is_r
        self.ch = chunk_rows(self.r, not row_is_r)
        self.tiles = (kloc + 127) // LANES
        self.kr = (self.tiles + SUB) // SUB * SUB
        self.nmax = max(n for _, n in self.ch)
        self.cut = [self.ch[i][0] for i in range(0, NCH, 2)] + [self.r]
        self.keep = not row_is_r


def rcopy(src, dst, sems, dev):
    if sems[0].shape:
        ref, *at = sems
        sems = ref.at[(0, *at)], ref.at[(1, *at)]
    return pltpu.make_async_remote_copy(src_ref=src, dst_ref=dst, send_sem=sems[0], recv_sem=sems[1], device_id=dev, device_id_type=MESH)


def places():
    dp = lax.axis_index('dp')
    c, chip = lax.rem(dp, 2), lax.div(dp, 2)
    x, y = lax.rem(chip, 2), lax.div(chip, 2)
    return dp, c, chip, chip + 1 - 2 * x, chip + 2 - 4 * y, 3 - chip


def main_kernel(mats, sh, *refs):
    it = iter(refs)
    lr_ref, wd_ref, b2_ref = next(it), next(it), next(it)
    for m in mats:
        m.g, m.w, m.mom, m.row_arg, m.col_arg = (next(it) for _ in range(5))
    for m in mats:
        (m.ag, m.mom_new, m.row_out, m.col_out, m.d2d, m.xy1, m.x2, m.y2, *m.far) = (next(it) for _ in range(12))
    stage, wst, usq, ucol = next(it), next(it), next(it), next(it)
    ld_sem, w_sem = next(it), next(it)
    for m in mats:
        (m.p, m.gt, m.gn, m.mv, m.colacc, m.msg, m.slots, m.rp, m.rz, m.sc, m.slots2, m.row_raw, m.col_raw, m.row_old, m.row_new, m.col_old, m.col_new) = (next(it) for _ in range(17))
        (m.d2d_s, m.rs1_s, m.x2_s, m.y2_s, m.ex_s, m.msg_s, m.z_s, m.sc_s, m.agx_s, m.agy_s, m.agd_s, m.ags_s, m.loc_s) = (next(it) for _ in range(13))
    tp = lax.axis_index('tp')
    dp, c, chip, jx, jy, jd = places()
    qx, qy, qd, qs = 2 * jx + c, 2 * jy + c, 2 * jd + c, dp + 1 - 2 * c
    sib, xn, yn = {'tp': tp, 'dp': qs}, {'tp': tp, 'dp': qx}, {'tp': tp, 'dp': qy}
    zn = {'tp': 1 - tp, 'dp': dp}
    me16 = tp * DP + dp

    sends = []

    def start(cp):
        cp.start()
        sends.append(cp)

    def d2d_copy(m, i):
        r0, n = m.ch[i]
        return rcopy(m.g.at[pl.ds(4 * (1 - c), 4), pl.ds(r0, n), :], m.d2d.at[:, pl.ds(r0, n), :], (m.d2d_s, i), sib)

    def own_load(m, i, b):
        r0, n = m.ch[i]
        return pltpu.make_async_copy(m.g.at[pl.ds(4 * c, 4), pl.ds(r0, n), :], stage.at[b, 0, :, pl.ds(0, n), :], ld_sem.at[b, 0])

    def got_load(m, i, b):
        r0, n = m.ch[i]
        return pltpu.make_async_copy(m.d2d.at[:, pl.ds(r0, n), :], stage.at[b, 1, :, pl.ds(0, n), :], ld_sem.at[b, 1])

    def pack_chunk(m, i, b):
        r0, n = m.ch[i]
        own_load(m, i, b).wait()
        got_load(m, i, b).wait()

        def body(t, carry):
            rs = pl.multiple_of(t * SUB, SUB)
            rd = pl.multiple_of(r0 + t * SUB, SUB)
            xs = [stage[b, 0, k, pl.ds(rs, SUB), :] + stage[b, 1, k, pl.ds(rs, SUB), :] for k in range(4)]
            for j in range(4):
                parts = [xs[k][:, sh * (2 * j + cc):sh * (2 * j + cc + 1)] for cc in range(2) for k in range(4)]
                m.p[j, pl.ds(rd, SUB), :] = jnp.concatenate(parts, axis=1)
            return carry

        lax.fori_loop(0, n // SUB, body, 0)

    def pview(m, j, i):
        r0, n = m.ch[i]
        return m.p.at[j, pl.ds(r0, n), :]

    def hview(ref, m, i):
        r0, n = m.ch[i]
        return ref.at[pl.ds(r0, n), :]

    def rs1_copy(m, i):
        dev = xn if i < 4 else yn
        return rcopy(pview(m, jd, i), hview(m.xy1, m, i), (m.rs1_s, i), dev)

    def x2_copy(m, i):
        return rcopy(pview(m, jx, i), hview(m.x2, m, i), (m.x2_s, i), xn)

    def y2_copy(m, i):
        return rcopy(pview(m, jy, i), hview(m.y2, m, i), (m.y2_s, i), yn)

    def rs_free(m, i):
        start(x2_copy(m, i) if i < 4 else y2_copy(m, i))

    def rs_pack(m, send):
        own_load(m, ORDER[0], 0).start()
        for s, i in enumerate(ORDER):
            d2d_copy(m, i).wait_recv()
            got_load(m, i, s % 2).start()
            if s + 1 < NCH:
                own_load(m, ORDER[s + 1], (s + 1) % 2).start()
            pack_chunk(m, i, s % 2)
            if send:
                start(rs1_copy(m, i))
                if s < 4:
                    rs_free(m, i)

    def rs_dep(m, ids):
        def load(s):
            i = ids[s]
            _, n = m.ch[i]
            return pltpu.make_async_copy(hview(m.xy1, m, i), stage.at[s % 2, 0, 0, pl.ds(0, n), :], ld_sem.at[s % 2, 0])

        for s, i in enumerate(ids):
            r0, n = m.ch[i]
            rs1_copy(m, i).wait_recv()
            load(s).start()
            load(s).wait()
            j = jy if i < 4 else jx

            def body(t, carry):
                rs = pl.multiple_of(t * SUB, SUB)
                rd = pl.multiple_of(r0 + t * SUB, SUB)
                m.p[j, pl.ds(rd, SUB), :] = m.p[j, pl.ds(rd, SUB), :] + stage[s % 2, 0, 0, pl.ds(rs, SUB), :]
                return carry

            lax.fori_loop(0, n // SUB, body, 0)
            start(y2_copy(m, i) if i < 4 else x2_copy(m, i))

    def acc_own(m, ids):
        base = (2 * c * (4 * m.r), (2 - c) * (4 * m.r))

        def loads(s):
            i = ids[s]
            _, n = m.ch[i]
            b = s % 2
            return (pltpu.make_async_copy(hview(m.x2, m, i), stage.at[b, 0, 0, pl.ds(0, n), :], ld_sem.at[b, 0]),
                    pltpu.make_async_copy(hview(m.y2, m, i), stage.at[b, 0, 1, pl.ds(0, n), :], ld_sem.at[b, 1]))

        for s, i in enumerate(ids):
            r0, n = m.ch[i]
            b = s % 2
            x2_copy(m, i).wait_recv()
            y2_copy(m, i).wait_recv()
            la, lb = loads(s)
            la.start()
            lb.start()
            la.wait()
            lb.wait()

            def body(t, carry):
                rs = pl.multiple_of(t * SUB, SUB)
                rd = pl.multiple_of(r0 + t * SUB, SUB)
                v = m.p[chip, pl.ds(rd, SUB), :] + stage[b, 0, 0, pl.ds(rs, SUB), :] + stage[b, 0, 1, pl.ds(rs, SUB), :]
                for cc in range(2):
                    for k in range(4):
                        row = pl.multiple_of(base[cc] + k * m.r + r0 + t * SUB, SUB)
                        m.gt[pl.ds(row, SUB), 0:sh] = v[:, sh * (4 * cc + k):sh * (4 * cc + k + 1)]
                return carry

            lax.fori_loop(0, n // SUB, body, 0)

    def ex_copy(m):
        h = 4 * m.r
        return rcopy(m.gt.at[pl.ds(2 * h, h), :], m.gt.at[pl.ds(c * h, h), :], (m.ex_s,), sib)

    def ex_wait(m):
        h = 4 * m.r
        rcopy(m.gt.at[pl.ds(2 * h, h), :], m.gt.at[pl.ds((1 - c) * h, h), :], (m.ex_s,), sib).wait_recv()

    def to_gn(m):
        full = m.k // LANES

        def body(t, carry):
            o = pl.multiple_of(t * LANES, LANES)
            m.gn[:, pl.ds(o, LANES)] = m.gt[pl.ds(o, LANES), :].T[0:sh, :]
            return carry

        lax.fori_loop(0, full, body, 0)
        rest = m.k - full * LANES
        if rest:
            m.gn[:, full * LANES:m.k] = m.gt[full * LANES:full * LANES + LANES, :].T[0:sh, 0:rest]

    def from_gn(m):
        full = m.k // LANES
        pad = m.gt.shape[1] - sh

        def turn(v):
            return jnp.concatenate([v, jnp.zeros((pad, LANES), F32)], axis=0).T

        def body(t, carry):
            o = pl.multiple_of(t * LANES, LANES)
            m.gt[pl.ds(o, LANES), :] = turn(m.gn[:, pl.ds(o, LANES)])
            return carry

        lax.fori_loop(0, full, body, 0)
        rest = m.k - full * LANES
        if rest:
            v = jnp.concatenate([m.gn[:, full * LANES:m.k], jnp.zeros((sh, LANES - rest), F32)], axis=1)
            m.gt[full * LANES:m.k, :] = turn(v)[0:rest, :]

    def vec_loads(m):
        return (pltpu.make_async_copy(m.row_arg, m.row_raw.at[pl.ds(0, 1), :], m.loc_s.at[3]),
                pltpu.make_async_copy(m.col_arg, m.col_raw.at[pl.ds(0, 1), :], m.loc_s.at[4]))

    def vec_stores(m):
        return (pltpu.make_async_copy(m.row_raw.at[pl.ds(0, 1), :], m.row_out, m.loc_s.at[3]),
                pltpu.make_async_copy(m.col_raw.at[pl.ds(0, 1), :], m.col_out, m.loc_s.at[4]))

    def vec_prepare(m):
        for cp in vec_loads(m):
            cp.wait()
        pad = m.gt.shape[1] - sh
        row = jnp.concatenate([m.row_raw[0:1, :], jnp.zeros((1, pad), F32)], axis=1)
        m.row_old[...] = jnp.broadcast_to(row, (LANES, sh + pad)).T[0:sh, :]
        m.col_old[...] = jnp.zeros_like(m.col_old)
        for t in range(m.tiles):
            w = min(LANES, m.k - LANES * t)
            m.col_old[t:t + 1, 0:w] = m.col_raw[0:1, LANES * t:LANES * t + w]

    def vec_finish(m):
        pad = m.gt.shape[1] - sh
        m.row_raw[...] = jnp.concatenate([m.row_new[...], jnp.zeros((pad, LANES), F32)], axis=0).T[0:SUB, 0:sh]
        for t in range(m.tiles):
            w = min(LANES, m.k - LANES * t)
            m.col_raw[0:1, LANES * t:LANES * t + w] = m.col_new[t:t + 1, 0:w]
        for cp in vec_stores(m):
            cp.start()

    def peers():
        out = []
        for d in range(1, DP):
            q = lax.rem(dp + d, DP)
            out.append((YES, tp, q))
        for d in range(DP):
            q = lax.rem(dp + d, DP)
            out.append((NO, 1 - tp, q))
        return out

    def msg_copies(m, sending):
        out = []
        for n, (same, t, q) in enumerate(peers()):
            slot = me16 if sending else t * SUB + q
            dev = {'tp': t, 'dp': q}
            sems = m.msg_s.at[0, n], m.msg_s.at[1, slot]
            rows = pl.ds(0, m.tiles + 1) if same else pl.ds(m.tiles, 1)
            out.append(rcopy(m.msg.at[rows, :], m.slots.at[slot, rows, :], sems, dev))
        return out

    def z_copy(m):
        return rcopy(m.rp, m.rz, (m.z_s,), zn)

    def sc_copies(m, sending):
        out = []
        for n, (same, t, q) in enumerate(peers()):
            slot = me16 if sending else t * SUB + q
            out.append(rcopy(m.sc.at[pl.ds(0, 1), :], m.slots2.at[slot, pl.ds(0, 1), :], (m.sc_s.at[0, n], m.sc_s.at[1, slot]), {'tp': t, 'dp': q}))
        return out

    def stats1(m):
        b2 = b2_ref[0]
        m.colacc[...] = jnp.zeros_like(m.colacc)

        def body(t, carry):
            rr = pl.multiple_of(t * SUB, SUB)
            rsum = jnp.zeros((DP, 1), F32)
            for s0, w in lane_chunks(m.k):
                g = m.gn[pl.ds(rr, SUB), s0:s0 + w]
                sq = g * g + 1e-30
                m.colacc[:, s0:s0 + w] = m.colacc[:, s0:s0 + w] + sq
                rsum = rsum + jnp.sum(sq, axis=1, keepdims=YES)
            m.rp[pl.ds(rr, SUB), :] = jnp.broadcast_to(rsum, (SUB, LANES))
            return carry

        lax.fori_loop(0, sh // SUB, body, 0)
        for i in range(m.tiles):
            w = min(LANES, m.k - LANES * i)
            m.msg[i:i + 1, 0:w] = jnp.sum(m.colacc[:, LANES * i:LANES * i + w], axis=0, keepdims=YES)
        mean_s = jnp.sum(m.rp[...] * (1.0 / m.ktot), axis=0, keepdims=YES) * (1.0 / m.width)
        if m.row_is_r:
            old = jnp.sum(m.row_old[...], axis=0, keepdims=YES) * (0.5 / m.width)
        else:
            old = jnp.sum(jnp.sum(m.col_old[...], axis=0, keepdims=YES), axis=1, keepdims=YES) * (0.125 / m.ktot)
        m.msg[m.tiles:m.tiles + 1, :] = jnp.broadcast_to(b2 * old + (1.0 - b2) * mean_s, (1, LANES))
        m.slots[me16, :, :] = m.msg[...]
        for cp in msg_copies(m, YES):
            start(cp)
        start(z_copy(m))

    def stats2(m):
        b2 = b2_ref[0]
        for cp in msg_copies(m, NO):
            cp.wait_recv()
        z_copy(m).wait_recv()
        tot = m.slots[tp * DP, 0:m.kr, :]
        for q in range(1, DP):
            tot = tot + m.slots[tp * DP + q, 0:m.kr, :]
        m.col_new[...] = b2 * m.col_old[...] + (1.0 - b2) * (tot / float(m.width))
        m.row_new[...] = b2 * m.row_old[...] + (1.0 - b2) * ((m.rp[...] + m.rz[...]) / float(m.ktot))
        mean_r = m.slots[0, m.tiles:m.tiles + 1, :]
        for q in range(1, EVERY):
            mean_r = mean_r + m.slots[q, m.tiles:m.tiles + 1, :]
        mean_r = mean_r[:, 0:1]
        usq[...] = jnp.zeros_like(usq)
        ucol[...] = jnp.zeros_like(ucol)

        def body(t, carry):
            rr = pl.multiple_of(t * SUB, SUB)
            rv = m.row_new[pl.ds(rr, SUB), 0:1]
            acc = jnp.zeros((DP, 1), F32)
            for i in range(m.tiles):
                s0, w = LANES * i, min(LANES, m.k - LANES * i)
                second = rv * m.col_new[i:i + 1, 0:w] / mean_r
                u = m.gn[pl.ds(rr, SUB), s0:s0 + w] / jnp.sqrt(second)
                m.gn[pl.ds(rr, SUB), s0:s0 + w] = u
                if w == LANES:
                    usq[...] = usq[...] + u * u
                else:
                    acc = acc + jnp.sum(u * u, axis=1, keepdims=YES)
            ucol[...] = ucol[...] + jnp.broadcast_to(acc, (SUB, LANES))
            return carry

        lax.fori_loop(0, sh // SUB, body, 0)
        usum = jnp.sum(jnp.sum(usq[...], axis=1, keepdims=YES), axis=0, keepdims=YES)
        usum = usum + jnp.sum(ucol[:, 0:1], axis=0, keepdims=YES)
        m.sc[...] = jnp.broadcast_to(usum, (SUB, LANES))
        m.slots2[me16, :, :] = m.sc[...]
        for cp in sc_copies(m, YES):
            start(cp)

    def stats2_end(m):
        for cp in sc_copies(m, NO):
            cp.wait_recv()

    def stats3(m):
        tot = m.slots2[0, 0:1, :]
        for q in range(1, EVERY):
            tot = tot + m.slots2[q, 0:1, :]
        den = jnp.maximum(1.0, jnp.sqrt(tot / (float(m.width) * float(m.ktot))))[0:1, 0:1]
        mom_load(m).wait()

        def body(t, carry):
            rr = pl.multiple_of(t * 16, 16)
            for s0, w in lane_chunks(m.k):
                u = m.gn[pl.ds(rr, 16), s0:s0 + w] / den
                mn = (0.9 * m.mv[pl.ds(rr, 16), s0:s0 + w].astype(F32) + 0.1 * u).astype(BF16)
                m.mv[pl.ds(rr, 16), s0:s0 + w] = mn
                m.gn[pl.ds(rr, 16), s0:s0 + w] = mn.astype(F32)
            return carry

        lax.fori_loop(0, sh // 16, body, 0)
        mom_store(m).start()
        from_gn(m)

    def mom_load(m):
        return pltpu.make_async_copy(m.mom, m.mv, m.loc_s.at[0])

    def mom_store(m):
        return pltpu.make_async_copy(m.mv, m.mom_new, m.loc_s.at[1])

    def own_copy(m):
        return pltpu.make_async_copy(m.p.at[chip], m.ag.at[dp], m.loc_s.at[2])

    lane0 = jnp.minimum(lax.div(sh * dp, LANES), DP)
    off = sh * dp - lane0 * LANES

    def w_load(m, i, b):
        r0, n = m.ch[i]
        return pltpu.make_async_copy(m.w.at[:, pl.ds(r0, n), pl.ds(pl.multiple_of(lane0 * LANES, LANES), WINDOW)], wst.at[b, :, pl.ds(0, n), :], w_sem.at[b])

    def new_weights(m, sent):
        lr, wd = lr_ref[0], wd_ref[0]
        w_load(m, 0, 0).start()
        for i in range(NCH):
            r0, n = m.ch[i]
            b = i % 2
            if i + 1 < NCH:
                w_load(m, i + 1, 1 - b).start()
            w_load(m, i, b).wait()

            def body(t, carry):
                rs = pl.multiple_of(t * SUB, SUB)
                rd = pl.multiple_of(r0 + t * SUB, SUB)
                heads, tails = [], []
                for k in range(DP):
                    w = pltpu.roll(wst[b, k, pl.ds(rs, SUB), :], lax.rem(WINDOW - off, WINDOW), 1)[:, 0:sh]
                    mt = m.gt[pl.ds(pl.multiple_of(k * m.r + r0 + t * SUB, SUB), DP), 0:sh]
                    new = w - lr * mt - lr * wd * w
                    heads.append(pltpu.roll(new[:, 0:LANES], lax.rem(sh * dp, LANES), 1))
                    tails.append(new[:, LANES:sh])
                m.p[chip, pl.ds(rd, SUB), :] = jnp.concatenate(heads + tails, axis=1)
                return carry

            lax.fori_loop(0, n // SUB, body, 0)
            if i < sent:
                ag_own(m, i)

    def agrow(m, q, i):
        r0, n = m.ch[i]
        return m.ag.at[q, pl.ds(r0, n), :]

    def kept(m, i):
        r0, n = m.ch[i]
        return m.far[i // 2].at[pl.ds(r0 - m.cut[i // 2], n), :]

    def xrow(m, q, i):
        return kept(m, i) if m.keep and i < 4 else agrow(m, q, i)

    def yrow(m, q, i):
        return kept(m, i) if m.keep and i >= 4 else agrow(m, q, i)

    def ag_own(m, i):
        start(rcopy(pview(m, chip, i), xrow(m, dp, i), (m.agx_s, i), xn))
        start(rcopy(pview(m, chip, i), yrow(m, dp, i), (m.agy_s, i), yn))

    def ag_sib_own(m, i):
        start(rcopy(pview(m, chip, i), agrow(m, dp, i), (m.ags_s, 0, i), sib))

    def ag_sib(m, which, src, q, i):
        start(rcopy(src, agrow(m, q, i), (m.ags_s, which, i), sib))

    def ag_xy(m, i):
        fx, fy = xrow(m, qx, i), yrow(m, qy, i)
        rcopy(fx, fx, (m.agx_s, i), xn).wait_recv()
        rcopy(fy, fy, (m.agy_s, i), yn).wait_recv()
        if not m.keep:
            if i < 4:
                start(rcopy(fx, fx, (m.agd_s, i), yn))
            else:
                start(rcopy(fy, fy, (m.agd_s, i), xn))
        ag_sib(m, 1, fx, qx, i)
        ag_sib(m, 2, fy, qy, i)

    def ag_d(m, i):
        rcopy(agrow(m, qd, i), agrow(m, qd, i), (m.agd_s, i), xn).wait_recv()
        ag_sib(m, 3, agrow(m, qd, i), qd, i)

    def ag_end(m):
        blocks = (qs, qx + 1 - 2 * c, qy + 1 - 2 * c, qd + 1 - 2 * c)
        for which, q in enumerate(blocks[0:3] if m.keep else blocks):
            for i in range(NCH):
                rcopy(agrow(m, q, i), agrow(m, q, i), (m.ags_s, which, i), sib).wait_recv()

    a, o = mats
    for i in ORDER:
        start(d2d_copy(a, i))
    rs_pack(a, YES)
    for i in ORDER[4:]:
        rs_free(a, i)
    for i in ORDER:
        start(d2d_copy(o, i))
    for m in mats:
        mom_load(m).start()
        for cp in vec_loads(m):
            cp.start()
    rs_dep(a, ORDER)
    rs_pack(o, NO)
    for m in mats:
        vec_prepare(m)
    for i in ORDER[0:6]:
        start(rs1_copy(o, i))
    acc_own(a, ORDER)
    start(ex_copy(a))
    for i in ORDER[6:]:
        start(rs1_copy(o, i))
    for i in ORDER[0:2]:
        rs_free(o, i)
    ex_wait(a)
    to_gn(a)
    stats1(a)
    for i in ORDER[2:4]:
        rs_free(o, i)
    stats2(a)
    for i in ORDER[4:6]:
        rs_free(o, i)
    stats2_end(a)
    for i in ORDER[6:]:
        rs_free(o, i)
    rs_dep(o, ORDER)
    stats3(a)
    new_weights(a, 3)
    vec_finish(a)
    own_copy(a).start()
    for i in range(NCH):
        ag_sib_own(a, i)
    acc_own(o, ORDER)
    start(ex_copy(o))
    ex_wait(o)
    to_gn(o)
    stats1(o)
    for i in range(3, 5):
        ag_own(a, i)
    stats2(o)
    ag_own(a, 5)
    stats2_end(o)
    for i in range(6, NCH):
        ag_own(a, i)
    stats3(o)
    new_weights(o, 0)
    vec_finish(o)
    own_copy(o).start()
    for i in range(NCH):
        ag_sib_own(o, i)
    for i in range(NCH):
        ag_xy(a, i)
    for i in range(NCH):
        ag_own(o, i)
    for i in range(NCH):
        ag_d(a, i)
    for i in range(NCH):
        ag_xy(o, i)
    for m in mats:
        ag_end(m)
        own_copy(m).wait()
        mom_store(m).wait()
        for cp in vec_stores(m):
            cp.wait()
    for cp in sends:
        cp.wait_send()


def split_rows(rows, parts):
    tiles = rows // SUB
    inner = tiles - 4
    out, start = [], 0
    for n in [2] + [inner // parts + (1 if i < inner % parts else 0) for i in range(parts)] + [2]:
        out.append((SUB * start, SUB * n))
        start += n
    return out


def turn_rows(sh, src, dst, row, rows):
    extra = sh - LANES
    tiles = DP * sh // LANES

    def tile(t):
        return pl.ds(LANES * t, LANES)

    def body(t, carry):
        lane = lax.broadcasted_iota(jnp.int32, (SUB, LANES), 1)
        rs = pl.ds(pl.multiple_of(row + t * SUB, SUB), SUB)
        rd = pl.ds(pl.multiple_of(t * SUB, SUB), SUB)
        ends = [[src[q, rs, tile(e)] for e in range(DP, tiles)] for q in range(DP)]
        for k in range(DP):
            out = [None] * tiles

            def place(v, lo, hi):
                for e in range(lo // LANES, (hi - 1) // LANES + 1):
                    at = max(lo - LANES * e, 0)
                    out[e] = v if out[e] is None else jnp.where(lane >= at, v, out[e])

            first, last = extra * k // LANES, (extra * (k + 1) - 1) // LANES
            for q in range(DP):
                place(src[q, rs, tile(k)], sh * q, sh * q + LANES)
                v = ends[q][first]
                if last > first:
                    v = jnp.where(lane >= extra * k % LANES, v, ends[q][last])
                turn = extra * (q - k) % LANES
                if turn:
                    v = pltpu.roll(v, turn, 1)
                place(v, sh * q + LANES, sh * (q + 1))
            for e in range(tiles):
                dst[k, rd, tile(e)] = out[e]
        return carry

    lax.fori_loop(0, rows // SUB, body, 0)


def unpack_in_kernel(sh, work, count, src, *refs):
    small, dst, small_out = refs[0:count], refs[count], refs[count + 1:2 * count + 1]
    src_v, dst_v, in_sem, out_sem, small_sem, *small_v = refs[2 * count + 1:]
    ins, outs = src_v.shape[0], dst_v.shape[0]

    def load(s):
        r0, n = work[s]
        return pltpu.make_async_copy(src.at[:, pl.ds(r0, n), :], src_v.at[s % ins, :, pl.ds(0, n), :], in_sem.at[s % ins])

    def store(s):
        r0, n = work[s]
        return pltpu.make_async_copy(dst_v.at[s % outs, :, pl.ds(0, n), :], dst.at[:, pl.ds(r0, n), :], out_sem.at[s % outs])

    def small_in(k):
        return pltpu.make_async_copy(small[k], small_v[k], small_sem.at[0, k])

    def small_back(k):
        return pltpu.make_async_copy(small_v[k], small_out[k], small_sem.at[1, k])

    for s in range(ins - 1):
        load(s).start()
    for k in range(count):
        small_in(k).start()
    for s, (r0, n) in enumerate(work):
        if s + ins - 1 < len(work):
            load(s + ins - 1).start()
        load(s).wait()
        if s >= outs:
            store(s - outs).wait()
        turn_rows(sh, src_v.at[s % ins], dst_v.at[s % outs], 0, n)
        store(s).start()
        if s == ins:
            for k in range(count):
                small_in(k).wait()
                small_back(k).start()
    for s in range(len(work) - outs, len(work)):
        store(s).wait()
    for k in range(count):
        small_back(k).wait()


def early_kernel(cut, ag, *refs):
    far, hold, sem = refs[0:4], refs[4], refs[5]
    dp, c, chip, *chips = places()
    qx, qy, _ = (2 * j + c for j in chips)
    other = 1 - 2 * c
    rows = [pl.ds(lo, hi - lo) for lo, hi in zip(cut, cut[1:])]
    copies = [(ag.at[q], hold.at[q]) for q in (dp, dp + other, qx + other, qy + other)]
    for e, part in enumerate(rows):
        for q, near in ((qx, e >= 2), (qy, e < 2)):
            copies.append((ag.at[q, part, :] if near else far[e], hold.at[q, part, :]))
    copies = [pltpu.make_async_copy(v, w, sem.at[e]) for e, (v, w) in enumerate(copies)]
    for cp in copies:
        cp.start()
    for cp in copies:
        cp.wait()


def late_kernel(sh, work, firsts, *refs):
    late, (dst, hold, dst_v, in_sem, out_sem) = refs[1:5], refs[-5:]
    *_, c, _, _, _, jd = places()
    outs = dst_v.shape[0]

    def loads(s):
        r0, n = work[s]
        half = int(r0 >= firsts[1])
        blocks = 2 * jd + c, 2 * jd + 1 - c
        part = pl.ds(r0 - firsts[half], n)
        return [pltpu.make_async_copy(late[2 * e + half].at[part, :], hold.at[q, pl.ds(r0, n), :], in_sem.at[s, e]) for e, q in enumerate(blocks)]

    def store(s):
        r0, n = work[s]
        return pltpu.make_async_copy(dst_v.at[s % outs, :, pl.ds(0, n), :], dst.at[:, pl.ds(r0, n), :], out_sem.at[s % outs])

    for s in range(len(work)):
        for cp in loads(s):
            cp.start()
    for s, (r0, n) in enumerate(work):
        for cp in loads(s):
            cp.wait()
        if s >= outs:
            store(s - outs).wait()
        turn_rows(sh, hold, dst_v.at[s % outs], r0, n)
        store(s).start()
    for s in range(len(work) - outs, len(work)):
        store(s).wait()


IN_HBM = pl.BlockSpec(memory_space=pl.ANY)
IN_VMEM = pl.BlockSpec(memory_space=pltpu.VMEM)


def costing(size):
    return pl.CostEstimate(flops=1000 * size, bytes_accessed=DP * size, transcendentals=0)


def unpack_in(packed, small, sh):
    work = split_rows(packed.shape[1], 13)
    nmax = max(n for _, n in work)
    count = len(small)
    dma = pltpu.SemaphoreType.DMA
    buf = (DP, nmax, packed.shape[2])
    return pl.pallas_call(
        lambda *refs: unpack_in_kernel(sh, work, count, *refs),
        in_specs=[IN_HBM] * (1 + count),
        out_specs=[IN_HBM] * (1 + count),
        out_shape=[jax.ShapeDtypeStruct(v.shape, v.dtype) for v in (packed, *small)],
        scratch_shapes=[pltpu.VMEM((4, *buf), F32), pltpu.VMEM((3, *buf), F32), dma((4,)), dma((3,)), dma((2, count))]
        + [pltpu.VMEM(v.shape, v.dtype) for v in small],
        compiler_params=pltpu.CompilerParams(vmem_limit_bytes=ALL_VMEM),
        cost_estimate=costing(packed.size),
        name='unpack_in',
    )(packed, *small)


def early_out(ag, far, cut):
    return pl.pallas_call(
        lambda *refs: early_kernel(cut, *refs),
        in_specs=[IN_HBM] * (1 + len(far)),
        out_specs=IN_VMEM,
        out_shape=pltpu.VMEM(ag.shape, F32),
        scratch_shapes=[pltpu.SemaphoreType.DMA((12,))],
        compiler_params=pltpu.CompilerParams(vmem_limit_bytes=BESIDE_HOLD),
        cost_estimate=costing(ag.size),
        name='early_out',
    )(ag, *far)


def late_out(hold, late, firsts, sh, before=()):
    shape = hold.shape
    work = [(lo + r0, n) for lo, v in zip(firsts, late) for r0, n in split_rows(v.shape[0], 2)]
    nmax = max(n for _, n in work)
    dma = pltpu.SemaphoreType.DMA
    aliases = {0: 1, 5: 0} if before else {0: 1}
    return pl.pallas_call(
        lambda *refs: late_kernel(sh, work, firsts, *refs),
        in_specs=[IN_VMEM] + [IN_HBM] * (len(late) + len(before)),
        out_specs=[IN_HBM, IN_VMEM],
        out_shape=[jax.ShapeDtypeStruct(shape, F32), pltpu.VMEM(shape, F32)],
        input_output_aliases=aliases,
        scratch_shapes=[pltpu.VMEM((4, DP, nmax, shape[2]), F32), dma((len(work), 2)), dma((4,))],
        compiler_params=pltpu.CompilerParams(vmem_limit_bytes=BESIDE_HOLD),
        cost_estimate=costing(hold.size),
    )(hold, *late, *before)


def solution(mesh):
    tp_devs = mesh.shape['tp']

    def body(w_in, w_out, g_in, g_out, m_in, m_out, r_in, c_in, r_out, c_out, learn_rate, weight_decay, beta_two):
        width = w_in.shape[1]
        sh = width // DP
        mats = (Mat(w_in.shape[2], width, tp_devs, YES), Mat(w_out.shape[1], width, tp_devs, NO))
        a, o = mats

        def grouped(v, m):
            return v.reshape(DP, m.r, width)

        scal = [v.reshape(1) for v in (learn_rate, weight_decay, beta_two)]
        args = list(scal)
        args += [grouped(g_in[0, 0].T, a), grouped(w_in[0].T, a), m_in[0], r_in, c_in]
        args += [grouped(g_out[0, 0], o), grouped(w_out[0], o), m_out[0].T, c_out, r_out]
        sspec = pl.BlockSpec(memory_space=pltpu.SMEM)
        in_specs = [sspec] * 3 + [IN_HBM] * 10
        out_shape, out_specs = [], []
        for m in mats:
            big = jax.ShapeDtypeStruct((m.r, width), F32)
            out_shape += [jax.ShapeDtypeStruct((DP, m.r, width), F32), jax.ShapeDtypeStruct((sh, m.k), BF16),
                          jax.ShapeDtypeStruct((1, sh), F32), jax.ShapeDtypeStruct((1, m.k), F32),
                          jax.ShapeDtypeStruct((4, m.r, width), F32), big, big, big,
                          *(jax.ShapeDtypeStruct((hi - lo, width), F32) for lo, hi in zip(m.cut, m.cut[1:]))]
            out_specs += [IN_HBM] * 12
        nmax = max(m.nmax for m in mats)
        dma = pltpu.SemaphoreType.DMA
        scratch = [pltpu.VMEM((2, 2, 4, nmax, width), F32), pltpu.VMEM((2, DP, nmax, WINDOW), F32), pltpu.VMEM((SUB, LANES), F32), pltpu.VMEM((SUB, LANES), F32), dma((2, 2)), dma((2,))]
        for m in mats:
            gt_rows = 12 * m.r
            scratch += [pltpu.VMEM((4, m.r, width), F32), pltpu.VMEM((gt_rows, 256), F32), pltpu.VMEM((sh, LANES * m.tiles), F32),
                        pltpu.VMEM((sh, m.k), BF16), pltpu.VMEM((SUB, LANES * m.tiles), F32), pltpu.VMEM((m.kr, LANES), F32),
                        pltpu.VMEM((EVERY, m.kr, LANES), F32), pltpu.VMEM((sh, LANES), F32), pltpu.VMEM((sh, LANES), F32),
                        pltpu.VMEM((SUB, LANES), F32), pltpu.VMEM((EVERY, SUB, LANES), F32),
                        pltpu.VMEM((SUB, sh), F32), pltpu.VMEM((SUB, m.k), F32), pltpu.VMEM((sh, LANES), F32), pltpu.VMEM((sh, LANES), F32),
                        pltpu.VMEM((m.kr, LANES), F32), pltpu.VMEM((m.kr, LANES), F32)]
            scratch += [dma((2, NCH)), dma((2, NCH)), dma((2, NCH)), dma((2, NCH)), dma((2,)), dma((2, EVERY)), dma((2,)), dma((2, EVERY)),
                        dma((2, NCH)), dma((2, NCH)), dma((2, NCH)), dma((2, 4, NCH)), dma((5,))]
        outs = pl.pallas_call(
            lambda *refs: main_kernel(mats, sh, *refs),
            in_specs=in_specs,
            out_specs=out_specs,
            out_shape=out_shape,
            scratch_shapes=scratch,
            compiler_params=pltpu.CompilerParams(has_side_effects=YES, vmem_limit_bytes=ALL_VMEM),
            name='step',
        )(*args)
        first, second, far = outs[0:4], outs[12:16], outs[20:]
        chips = mesh.shape['dp'] // 2

        def swap(v, bit):
            return lax.ppermute(v, 'dp', [(q, q ^ bit) for q in range(2 * chips)])

        over = []
        for e in range(2):
            over.append((swap(far[e], 4), swap(far[2 + e], 2)))
        done = unpack_in(first[0], (*first[1:], *second[1:]), sh)
        *both, small = lax.optimization_barrier((*over[0], *far, done[2]))
        early, far = both[0:2], both[2:]
        across = [swap(v, 1) for v in early]
        hold = early_out(second[0], far, o.cut)
        *last, hold = lax.optimization_barrier((*over[1], hold))
        part, hold = late_out(hold, (*early, *across), (o.cut[0], o.cut[2]), sh)
        across = [swap(v, 1) for v in last]
        new_out, _ = late_out(hold, (*last, *across), (o.cut[1], o.cut[3]), sh, (part,))
        new_in = done[0].reshape(a.k, width).T[None]
        new_out = new_out.reshape(o.k, width)[None]
        mom_in, _, col_in, mom_out, row_out, col_out = done[1:]
        return (new_in, new_out, mom_in[None], mom_out.T[None], small, col_in, col_out, row_out)

    free = None
    rows_tp, cols_tp = P(free, 'tp', free), P(free, free, 'tp')
    on_dp, on_tp, whole = P(free, 'dp'), P(free, 'tp'), P()
    state_in, state_out = P(free, 'dp', 'tp'), P(free, 'tp', 'dp')
    in_specs = (cols_tp, rows_tp, P('dp', free, free, 'tp'), P('dp', free, 'tp', free), state_in, state_out, on_dp, on_tp, on_tp, on_dp, whole, whole, whole)
    out_specs = (cols_tp, rows_tp, state_in, state_out, on_dp, on_tp, on_tp, on_dp)
    return jax.shard_map(body, mesh=mesh, in_specs=in_specs, out_specs=out_specs, check_vma=NO)
```

profile of v0, /device:TPU:0, one launch (start us, length us, event | category | flops | bytes accessed | tf_op | source)
XLA Modules:
  0.0 456.0 jit_solution(7349918225853241365)
XLA Ops:
  2.6 400.4 %step.1 = (f32[8,648,1408]{2,1,0:T(8,128)}, bf16[176,5184]{1,0:T(8,128)(2,1)}, f32[1,176]{1,0:T(1,128)}, f32[1,5184]{1,0:T(1,128)}, f32[4,648,1408]{2,1,0:T(8,12...) custom-call(f32[1]{0:T(128)} %bitcast.29.refs_0_, ...), custom_call_target="tpu_custom_call" | custom-call | tf_op jit(solution)/shard_map/step/pallas_call | solution.py:807
  403.0 1.5 collective-permute-start.1
  404.5 0.6 collective-permute-start
  405.1 1.5 collective-permute-start.2
  406.5 0.6 collective-permute-start.3
  407.1 21.9 %unpack_in.1 = (f32[8,648,1408]{2,1,0:T(8,128)}, bf16[176,5184]{1,0:T(8,128)(2,1)}, f32[1,176]{1,0:T(1,128)}, f32[1,5184]{1,0:T(1,128)}, bf16[176,3776]{1,0:T(8,...) custom-call(f32[8,648,1408]{2,1,0:T(8,128)} %get-tuple-element.40.refs_0_, bf16[176,5184]{1,0:T(8,128)(2,1)} %get-tuple-element.41.refs_1_, ...), custom_call_target="tpu_custom_call" | custom-call | flops 7299072000 | bytes 58392576 | tf_op jit(solution)/shard_map/unpack_in/pallas_call | solution.py:724
  429.0 7.7 %collective-permute-done.2.refs_1_ = f32[120,1408]{1,0:T(8,128)} collective-permute-done((f32[120,1408]{1,0:T(8,128)}, f32[120,1408]{1,0:T(8,128)}, u32[]{:S(2)}, u32[]{:S(2)}) %collective-permute-start.2) | collective-permute-done | bytes 675872 | tf_op jit(solution)/shard_map/ppermute | solution.py:820
  436.8 0.0 collective-permute-done.3.refs_2_
  436.8 0.0 collective-permute-start.4
  436.8 0.5 collective-permute-start.5
  437.3 5.6 %early_out.1.refs_0_ = f32[8,472,1408]{2,1,0:T(8,128)S(1)} custom-call(f32[8,472,1408]{2,1,0:T(8,128)} %get-tuple-element.50.refs_0_, f32[120,1408]{1,0:T(8,128)} %get-tuple-element.54.refs_1_, f32[120,1408]{1,0:T(8,128)} %get-tuple-element.55.refs_2_, f32[120,1408]{1,0:T(8,128)} %get-tuple-element.56.refs_3_, f32[112,1408]{1,0:T(8,128)} %get-tuple-element.57.refs_4_), custom_call_target="tpu_custom_call" | custom-call | flops 5316608000 | bytes 42532864 | tf_op jit(solution)/shard_map/early_out/pallas_call | solution.py:738
  442.9 0.0 collective-permute-done.1.refs_2_
  442.9 0.0 collective-permute-done.refs_1_
  442.9 0.0 collective-permute-start.6
  443.0 0.5 collective-permute-start.7
  443.5 0.0 collective-permute-done.4.refs_3_
  443.5 0.0 collective-permute-done.5.refs_4_
  443.5 6.3 %shard_map.188 = (f32[8,472,1408]{2,1,0:T(8,128)}, f32[8,472,1408]{2,1,0:T(8,128)S(1)}) custom-call(f32[8,472,1408]{2,1,0:T(8,128)S(1)} %early_out.1.refs_0_, f32[120,1408]{1,0:T(8,128)} %collective-permute-done.2.refs_1_, f32[120,1408]{1,0:T(8,128)} %collective-permute-done.3.refs_2_, ...), custom_call_target="tpu_custom_call", output_to_operand_aliasing={{1}: (0, {})} | custom-call | flops 5316608000 | bytes 42532864 | tf_op jit(solution)/shard_map/pallas_call | solution.py:756
  449.8 0.0 collective-permute-done.7.refs_4_
  449.8 0.0 collective-permute-done.6.refs_3_
  449.8 6.2 %shard_map.189 = (f32[8,472,1408]{2,1,0:T(8,128)}, f32[8,472,1408]{2,1,0:T(8,128)S(1)}) custom-call(f32[8,472,1408]{2,1,0:T(8,128)S(1)} %get-tuple-element.61.refs_0_, f32[120,1408]{1,0:T(8,128)} %collective-permute-done.refs_1_, f32[112,1408]{1,0:T(8,128)} %collective-permute-done.1.refs_2_, ...), custom_call_target="tpu_custom_call", output_to_operand_aliasing={{1}: (0, {}), {0}: (5, {})} | custom-call | flops 5316608000 | bytes 42532864 | tf_op jit(solution)/shard_map/pallas_call | solution.py:756
Async XLA Ops:
  403.0 39.9 %collective-permute-start.1 = (f32[112,1408]{1,0:T(8,128)}, f32[112,1408]{1,0:T(8,128)}, u32[]{:S(2)}, u32[]{:S(2)}) collective-permute-start(f32[112,1408]{1,0:T(8,128)} %get-tuple-element.57.refs_4_), channel_id=1, source_target_pairs={{0,2},{1,3},{2,0},{3,1},{4,6},{5,7},{6,4},{7,5},{8,10},{9,11},{10,... | collective-permute-start | bytes 1892360 | tf_op jit(solution)/shard_map/ppermute | solution.py:820
  404.5 38.4 %collective-permute-start = (f32[120,1408]{1,0:T(8,128)}, f32[120,1408]{1,0:T(8,128)}, u32[]{:S(2)}, u32[]{:S(2)}) collective-permute-start(f32[120,1408]{1,0:T(8,128)} %get-tuple-element.55.refs_2_), channel_id=1, source_target_pairs={{0,4},{1,5},{2,6},{3,7},{4,0},{5,1},{6,2},{7,3},{8,12},{9,13},{10,... | collective-permute-start | bytes 2027528 | tf_op jit(solution)/shard_map/ppermute | solution.py:820
  405.1 31.7 %collective-permute-start.2 = (f32[120,1408]{1,0:T(8,128)}, f32[120,1408]{1,0:T(8,128)}, u32[]{:S(2)}, u32[]{:S(2)}) collective-permute-start(f32[120,1408]{1,0:T(8,128)} %get-tuple-element.54.refs_1_), channel_id=1, source_target_pairs={{0,4},{1,5},{2,6},{3,7},{4,0},{5,1},{6,2},{7,3},{8,12},{9,13},{10,... | collective-permute-start | bytes 2027528 | tf_op jit(solution)/shard_map/ppermute | solution.py:820
  406.5 30.3 %collective-permute-start.3 = (f32[120,1408]{1,0:T(8,128)}, f32[120,1408]{1,0:T(8,128)}, u32[]{:S(2)}, u32[]{:S(2)}) collective-permute-start(f32[120,1408]{1,0:T(8,128)} %get-tuple-element.56.refs_3_), channel_id=1, source_target_pairs={{0,2},{1,3},{2,0},{3,1},{4,6},{5,7},{6,4},{7,5},{8,10},{9,11},{10,... | collective-permute-start | bytes 2027528 | tf_op jit(solution)/shard_map/ppermute | solution.py:820
  436.8 6.7 %collective-permute-start.4 = (f32[120,1408]{1,0:T(8,128)}, f32[120,1408]{1,0:T(8,128)}, u32[]{:S(2)}, u32[]{:S(2)}) collective-permute-start(f32[120,1408]{1,0:T(8,128)} %collective-permute-done.2.refs_1_), channel_id=1, source_target_pairs={{0,1},{1,0},{2,3},{3,2},{4,5},{5,4},{6,7},{7,6},{8,9},{9,8},{10,11... | collective-permute-start | bytes 2027528 | tf_op jit(solution)/shard_map/ppermute | solution.py:820
  436.8 6.7 %collective-permute-start.5 = (f32[120,1408]{1,0:T(8,128)}, f32[120,1408]{1,0:T(8,128)}, u32[]{:S(2)}, u32[]{:S(2)}) collective-permute-start(f32[120,1408]{1,0:T(8,128)} %collective-permute-done.3.refs_2_), channel_id=1, source_target_pairs={{0,1},{1,0},{2,3},{3,2},{4,5},{5,4},{6,7},{7,6},{8,9},{9,8},{10,11... | collective-permute-start | bytes 2027528 | tf_op jit(solution)/shard_map/ppermute | solution.py:820
  442.9 6.8 %collective-permute-start.6 = (f32[120,1408]{1,0:T(8,128)}, f32[120,1408]{1,0:T(8,128)}, u32[]{:S(2)}, u32[]{:S(2)}) collective-permute-start(f32[120,1408]{1,0:T(8,128)} %collective-permute-done.refs_1_), channel_id=1, source_target_pairs={{0,1},{1,0},{2,3},{3,2},{4,5},{5,4},{6,7},{7,6},{8,9},{9,8},{10,11... | collective-permute-start | bytes 2027528 | tf_op jit(solution)/shard_map/ppermute | solution.py:820
  443.0 6.8 %collective-permute-start.7 = (f32[112,1408]{1,0:T(8,128)}, f32[112,1408]{1,0:T(8,128)}, u32[]{:S(2)}, u32[]{:S(2)}) collective-permute-start(f32[112,1408]{1,0:T(8,128)} %collective-permute-done.1.refs_2_), channel_id=1, source_target_pairs={{0,1},{1,0},{2,3},{3,2},{4,5},{5,4},{6,7},{7,6},{8,9},{9,8},{10,11... | collective-permute-start | bytes 1892360 | tf_op jit(solution)/shard_map/ppermute | solution.py:820
where the time goes:
time: 457 us; the launch traced here: 456 us
  Pallas kernels  440 us (96%)
  waiting for transfers between devices  7.76 us (2%)
  starting transfers between devices  5.14 us (1%)
    pallas_call x1, Pallas kernels, body(): pl.pallas_call(lambda *refs: main_kernel(mats, sh, *refs), in_specs=in_sp...  400 us
    pallas_call x1, Pallas kernels, unpack_in(): pl.pallas_call(lambda *refs: unpack_in_kernel(sh, work, count, *refs), in...  21.9 us
    pallas_call x2, Pallas kernels, late_out(): pl.pallas_call(lambda *refs: late_kernel(sh, work, firsts, *refs), in_spe...  12.4 us
  transfers between devices with their start and end apart: 8, of which 1 were waited for; matrix products, arithmetic and copies ran while one was open for 0% of the time, Pallas kernels for 7%

commit v1 on v0

--- a/solution.py
+++ b/solution.py
@@ -96,9 +96,13 @@
         cp.start()
         sends.append(cp)
 
+    def direct(m, i):
+        return m is mats[0] and i % 4 == 0
+
     def d2d_copy(m, i):
         r0, n = m.ch[i]
-        return rcopy(m.g.at[pl.ds(4 * (1 - c), 4), pl.ds(r0, n), :], m.d2d.at[:, pl.ds(r0, n), :], (m.d2d_s, i), sib)
+        dst = stage.at[i // 4, 1, :, pl.ds(0, n), :] if direct(m, i) else m.d2d.at[:, pl.ds(r0, n), :]
+        return rcopy(m.g.at[pl.ds(4 * (1 - c), 4), pl.ds(r0, n), :], dst, (m.d2d_s, i), sib)
 
     def own_load(m, i, b):
         r0, n = m.ch[i]
@@ -111,7 +115,8 @@
     def pack_chunk(m, i, b):
         r0, n = m.ch[i]
         own_load(m, i, b).wait()
-        got_load(m, i, b).wait()
+        if not direct(m, i):
+            got_load(m, i, b).wait()
 
         def body(t, carry):
             rs = pl.multiple_of(t * SUB, SUB)
@@ -149,7 +154,8 @@
         own_load(m, ORDER[0], 0).start()
         for s, i in enumerate(ORDER):
             d2d_copy(m, i).wait_recv()
-            got_load(m, i, s % 2).start()
+            if not direct(m, i):
+                got_load(m, i, s % 2).start()
             if s + 1 < NCH:
                 own_load(m, ORDER[s + 1], (s + 1) % 2).start()
             pack_chunk(m, i, s % 2)
@@ -726,7 +732,7 @@
         in_specs=[IN_HBM] * (1 + count),
         out_specs=[IN_HBM] * (1 + count),
         out_shape=[jax.ShapeDtypeStruct(v.shape, v.dtype) for v in (packed, *small)],
-        scratch_shapes=[pltpu.VMEM((4, *buf), F32), pltpu.VMEM((3, *buf), F32), dma((4,)), dma((3,)), dma((2, count))]
+        scratch_shapes=[pltpu.VMEM((6, *buf), F32), pltpu.VMEM((5, *buf), F32), dma((6,)), dma((5,)), dma((2, count))]
         + [pltpu.VMEM(v.shape, v.dtype) for v in small],
         compiler_params=pltpu.CompilerParams(vmem_limit_bytes=ALL_VMEM),
         cost_estimate=costing(packed.size),

time: 457 us -> 457 us (level)
  no operation moved by 1% of the time
where the time goes in v1:
time: 457 us; the launch traced here: 456 us
  Pallas kernels  440 us (96%)
  waiting for transfers between devices  7.7 us (2%)
  starting transfers between devices  5.14 us (1%)
    pallas_call x1, Pallas kernels, body(): pl.pallas_call(lambda *refs: main_kernel(mats, sh, *refs), in_specs=in_sp...  400 us
    pallas_call x1, Pallas kernels, unpack_in(): pl.pallas_call(lambda *refs: unpack_in_kernel(sh, work, count, *refs), in...  22 us
    pallas_call x2, Pallas kernels, late_out(): pl.pallas_call(lambda *refs: late_kernel(sh, work, firsts, *refs), in_spe...  12.4 us
  transfers between devices with their start and end apart: 8, of which 1 were waited for; matrix products, arithmetic and copies ran while one was open for 0% of the time, Pallas kernels for 7%

profile of v1, /device:TPU:0, one launch (start us, length us, event | category | flops | bytes accessed | tf_op | source)
XLA Modules:
  0.0 456.0 jit_solution(16431291734502673345)
XLA Ops:
  2.6 400.4 %step.1 = (f32[8,648,1408]{2,1,0:T(8,128)}, bf16[176,5184]{1,0:T(8,128)(2,1)}, f32[1,176]{1,0:T(1,128)}, f32[1,5184]{1,0:T(1,128)}, f32[4,648,1408]{2,1,0:T(8,12...) custom-call(f32[1]{0:T(128)} %bitcast.29.refs_0_, ...), custom_call_target="tpu_custom_call" | custom-call | tf_op jit(solution)/shard_map/step/pallas_call | solution.py:813
  403.0 1.5 collective-permute-start.1
  404.5 0.6 collective-permute-start
  405.1 1.5 collective-permute-start.2
  406.5 0.6 collective-permute-start.3
  407.1 22.0 %unpack_in.1 = (f32[8,648,1408]{2,1,0:T(8,128)}, bf16[176,5184]{1,0:T(8,128)(2,1)}, f32[1,176]{1,0:T(1,128)}, f32[1,5184]{1,0:T(1,128)}, bf16[176,3776]{1,0:T(8,...) custom-call(f32[8,648,1408]{2,1,0:T(8,128)} %get-tuple-element.40.refs_0_, bf16[176,5184]{1,0:T(8,128)(2,1)} %get-tuple-element.41.refs_1_, ...), custom_call_target="tpu_custom_call" | custom-call | flops 7299072000 | bytes 58392576 | tf_op jit(solution)/shard_map/unpack_in/pallas_call | solution.py:730
  429.1 7.7 %collective-permute-done.2.refs_1_ = f32[120,1408]{1,0:T(8,128)} collective-permute-done((f32[120,1408]{1,0:T(8,128)}, f32[120,1408]{1,0:T(8,128)}, u32[]{:S(2)}, u32[]{:S(2)}) %collective-permute-start.2) | collective-permute-done | bytes 675872 | tf_op jit(solution)/shard_map/ppermute | solution.py:826
  436.8 0.0 collective-permute-done.3.refs_2_
  436.8 0.0 collective-permute-start.4
  436.8 0.5 collective-permute-start.5
  437.3 5.6 %early_out.1.refs_0_ = f32[8,472,1408]{2,1,0:T(8,128)S(1)} custom-call(f32[8,472,1408]{2,1,0:T(8,128)} %get-tuple-element.50.refs_0_, f32[120,1408]{1,0:T(8,128)} %get-tuple-element.54.refs_1_, f32[120,1408]{1,0:T(8,128)} %get-tuple-element.55.refs_2_, f32[120,1408]{1,0:T(8,128)} %get-tuple-element.56.refs_3_, f32[112,1408]{1,0:T(8,128)} %get-tuple-element.57.refs_4_), custom_call_target="tpu_custom_call" | custom-call | flops 5316608000 | bytes 42532864 | tf_op jit(solution)/shard_map/early_out/pallas_call | solution.py:744
  442.9 0.0 collective-permute-done.1.refs_2_
  442.9 0.0 collective-permute-done.refs_1_
  442.9 0.0 collective-permute-start.6
  443.0 0.5 collective-permute-start.7
  443.5 0.0 collective-permute-done.4.refs_3_
  443.5 0.0 collective-permute-done.5.refs_4_
  443.5 6.3 %shard_map.188 = (f32[8,472,1408]{2,1,0:T(8,128)}, f32[8,472,1408]{2,1,0:T(8,128)S(1)}) custom-call(f32[8,472,1408]{2,1,0:T(8,128)S(1)} %early_out.1.refs_0_, f32[120,1408]{1,0:T(8,128)} %collective-permute-done.2.refs_1_, f32[120,1408]{1,0:T(8,128)} %collective-permute-done.3.refs_2_, ...), custom_call_target="tpu_custom_call", output_to_operand_aliasing={{1}: (0, {})} | custom-call | flops 5316608000 | bytes 42532864 | tf_op jit(solution)/shard_map/pallas_call | solution.py:762
  449.8 0.0 collective-permute-done.7.refs_4_
  449.8 0.0 collective-permute-done.6.refs_3_
  449.8 6.2 %shard_map.189 = (f32[8,472,1408]{2,1,0:T(8,128)}, f32[8,472,1408]{2,1,0:T(8,128)S(1)}) custom-call(f32[8,472,1408]{2,1,0:T(8,128)S(1)} %get-tuple-element.61.refs_0_, f32[120,1408]{1,0:T(8,128)} %collective-permute-done.refs_1_, f32[112,1408]{1,0:T(8,128)} %collective-permute-done.1.refs_2_, ...), custom_call_target="tpu_custom_call", output_to_operand_aliasing={{1}: (0, {}), {0}: (5, {})} | custom-call | flops 5316608000 | bytes 42532864 | tf_op jit(solution)/shard_map/pallas_call | solution.py:762
Async XLA Ops:
  403.0 39.9 %collective-permute-start.1 = (f32[112,1408]{1,0:T(8,128)}, f32[112,1408]{1,0:T(8,128)}, u32[]{:S(2)}, u32[]{:S(2)}) collective-permute-start(f32[112,1408]{1,0:T(8,128)} %get-tuple-element.57.refs_4_), channel_id=1, source_target_pairs={{0,2},{1,3},{2,0},{3,1},{4,6},{5,7},{6,4},{7,5},{8,10},{9,11},{10,... | collective-permute-start | bytes 1892360 | tf_op jit(solution)/shard_map/ppermute | solution.py:826
  404.5 38.4 %collective-permute-start = (f32[120,1408]{1,0:T(8,128)}, f32[120,1408]{1,0:T(8,128)}, u32[]{:S(2)}, u32[]{:S(2)}) collective-permute-start(f32[120,1408]{1,0:T(8,128)} %get-tuple-element.55.refs_2_), channel_id=1, source_target_pairs={{0,4},{1,5},{2,6},{3,7},{4,0},{5,1},{6,2},{7,3},{8,12},{9,13},{10,... | collective-permute-start | bytes 2027528 | tf_op jit(solution)/shard_map/ppermute | solution.py:826
  405.1 31.7 %collective-permute-start.2 = (f32[120,1408]{1,0:T(8,128)}, f32[120,1408]{1,0:T(8,128)}, u32[]{:S(2)}, u32[]{:S(2)}) collective-permute-start(f32[120,1408]{1,0:T(8,128)} %get-tuple-element.54.refs_1_), channel_id=1, source_target_pairs={{0,4},{1,5},{2,6},{3,7},{4,0},{5,1},{6,2},{7,3},{8,12},{9,13},{10,... | collective-permute-start | bytes 2027528 | tf_op jit(solution)/shard_map/ppermute | solution.py:826
  406.5 30.3 %collective-permute-start.3 = (f32[120,1408]{1,0:T(8,128)}, f32[120,1408]{1,0:T(8,128)}, u32[]{:S(2)}, u32[]{:S(2)}) collective-permute-start(f32[120,1408]{1,0:T(8,128)} %get-tuple-element.56.refs_3_), channel_id=1, source_target_pairs={{0,2},{1,3},{2,0},{3,1},{4,6},{5,7},{6,4},{7,5},{8,10},{9,11},{10,... | collective-permute-start | bytes 2027528 | tf_op jit(solution)/shard_map/ppermute | solution.py:826
  436.8 6.7 %collective-permute-start.4 = (f32[120,1408]{1,0:T(8,128)}, f32[120,1408]{1,0:T(8,128)}, u32[]{:S(2)}, u32[]{:S(2)}) collective-permute-start(f32[120,1408]{1,0:T(8,128)} %collective-permute-done.2.refs_1_), channel_id=1, source_target_pairs={{0,1},{1,0},{2,3},{3,2},{4,5},{5,4},{6,7},{7,6},{8,9},{9,8},{10,11... | collective-permute-start | bytes 2027528 | tf_op jit(solution)/shard_map/ppermute | solution.py:826
  436.8 6.7 %collective-permute-start.5 = (f32[120,1408]{1,0:T(8,128)}, f32[120,1408]{1,0:T(8,128)}, u32[]{:S(2)}, u32[]{:S(2)}) collective-permute-start(f32[120,1408]{1,0:T(8,128)} %collective-permute-done.3.refs_2_), channel_id=1, source_target_pairs={{0,1},{1,0},{2,3},{3,2},{4,5},{5,4},{6,7},{7,6},{8,9},{9,8},{10,11... | collective-permute-start | bytes 2027528 | tf_op jit(solution)/shard_map/ppermute | solution.py:826
  442.9 6.8 %collective-permute-start.6 = (f32[120,1408]{1,0:T(8,128)}, f32[120,1408]{1,0:T(8,128)}, u32[]{:S(2)}, u32[]{:S(2)}) collective-permute-start(f32[120,1408]{1,0:T(8,128)} %collective-permute-done.refs_1_), channel_id=1, source_target_pairs={{0,1},{1,0},{2,3},{3,2},{4,5},{5,4},{6,7},{7,6},{8,9},{9,8},{10,11... | collective-permute-start | bytes 2027528 | tf_op jit(solution)/shard_map/ppermute | solution.py:826
  443.0 6.8 %collective-permute-start.7 = (f32[112,1408]{1,0:T(8,128)}, f32[112,1408]{1,0:T(8,128)}, u32[]{:S(2)}, u32[]{:S(2)}) collective-permute-start(f32[112,1408]{1,0:T(8,128)} %collective-permute-done.1.refs_2_), channel_id=1, source_target_pairs={{0,1},{1,0},{2,3},{3,2},{4,5},{5,4},{6,7},{7,6},{8,9},{9,8},{10,11... | collective-permute-start | bytes 1892360 | tf_op jit(solution)/shard_map/ppermute | solution.py:826

commit v2 on v1

--- a/solution.py
+++ b/solution.py
@@ -501,6 +501,10 @@
                 rcopy(agrow(m, q, i), agrow(m, q, i), (m.ags_s, which, i), sib).wait_recv()
 
     a, o = mats
+    barrier = pltpu.get_barrier_semaphore()
+    for _, t, q in peers():
+        pl.semaphore_signal(barrier, inc=1, device_id={'tp': t, 'dp': q}, device_id_type=MESH)
+    pl.semaphore_wait(barrier, EVERY - 1)
     for i in ORDER:
         start(d2d_copy(a, i))
     rs_pack(a, YES)
@@ -816,7 +820,7 @@
             out_specs=out_specs,
             out_shape=out_shape,
             scratch_shapes=scratch,
-            compiler_params=pltpu.CompilerParams(has_side_effects=YES, vmem_limit_bytes=ALL_VMEM),
+            compiler_params=pltpu.CompilerParams(has_side_effects=YES, collective_id=0, vmem_limit_bytes=ALL_VMEM),
             name='step',
         )(*args)
         first, second, far = outs[0:4], outs[12:16], outs[20:]

time: 457 us -> 455 us (level)
  no operation moved by 1% of the time
where the time goes in v2:
time: 455 us; the launch traced here: 454 us
  Pallas kernels  439 us (96%)
  waiting for transfers between devices  6.78 us (1%)
  starting transfers between devices  5.14 us (1%)
    pallas_call x1, Pallas kernels, body(): pl.pallas_call(lambda *refs: main_kernel(mats, sh, *refs), in_specs=in_sp...  399 us
    pallas_call x1, Pallas kernels, unpack_in(): pl.pallas_call(lambda *refs: unpack_in_kernel(sh, work, count, *refs), in...  22 us
    pallas_call x2, Pallas kernels, late_out(): pl.pallas_call(lambda *refs: late_kernel(sh, work, firsts, *refs), in_spe...  12.4 us
  transfers between devices with their start and end apart: 8, of which 1 were waited for; matrix products, arithmetic and copies ran while one was open for 0% of the time, Pallas kernels for 7%

profile of v2, /device:TPU:0, one launch (start us, length us, event | category | flops | bytes accessed | tf_op | source)
XLA Modules:
  0.0 453.7 jit_solution(13533450032052134822)
XLA Ops:
  2.6 399.0 %step.1 = (f32[8,648,1408]{2,1,0:T(8,128)}, bf16[176,5184]{1,0:T(8,128)(2,1)}, f32[1,176]{1,0:T(1,128)}, f32[1,5184]{1,0:T(1,128)}, f32[4,648,1408]{2,1,0:T(8,12...) custom-call(f32[1]{0:T(128)} %bitcast.29.refs_0_, ...), custom_call_target="tpu_custom_call" | custom-call | tf_op jit(solution)/shard_map/step/pallas_call | solution.py:817
  401.6 0.6 collective-permute-start.1
  402.2 1.5 collective-permute-start
  403.7 0.5 collective-permute-start.2
  404.2 1.5 collective-permute-start.3
  405.7 22.0 %unpack_in.1 = (f32[8,648,1408]{2,1,0:T(8,128)}, bf16[176,5184]{1,0:T(8,128)(2,1)}, f32[1,176]{1,0:T(1,128)}, f32[1,5184]{1,0:T(1,128)}, bf16[176,3776]{1,0:T(8,...) custom-call(f32[8,648,1408]{2,1,0:T(8,128)} %get-tuple-element.40.refs_0_, bf16[176,5184]{1,0:T(8,128)(2,1)} %get-tuple-element.41.refs_1_, ...), custom_call_target="tpu_custom_call" | custom-call | flops 7299072000 | bytes 58392576 | tf_op jit(solution)/shard_map/unpack_in/pallas_call | solution.py:734
  427.7 6.8 %collective-permute-done.2.refs_1_ = f32[120,1408]{1,0:T(8,128)} collective-permute-done((f32[120,1408]{1,0:T(8,128)}, f32[120,1408]{1,0:T(8,128)}, u32[]{:S(2)}, u32[]{:S(2)}) %collective-permute-start.2) | collective-permute-done | bytes 675872 | tf_op jit(solution)/shard_map/ppermute | solution.py:830
  434.5 0.0 collective-permute-done.3.refs_2_
  434.5 0.0 collective-permute-start.4
  434.5 0.5 collective-permute-start.5
  435.0 5.6 %early_out.1.refs_0_ = f32[8,472,1408]{2,1,0:T(8,128)S(1)} custom-call(f32[8,472,1408]{2,1,0:T(8,128)} %get-tuple-element.50.refs_0_, f32[120,1408]{1,0:T(8,128)} %get-tuple-element.54.refs_1_, f32[120,1408]{1,0:T(8,128)} %get-tuple-element.55.refs_2_, f32[120,1408]{1,0:T(8,128)} %get-tuple-element.56.refs_3_, f32[112,1408]{1,0:T(8,128)} %get-tuple-element.57.refs_4_), custom_call_target="tpu_custom_call" | custom-call | flops 5316608000 | bytes 42532864 | tf_op jit(solution)/shard_map/early_out/pallas_call | solution.py:748
  440.6 0.0 collective-permute-done.1.refs_2_
  440.6 0.0 collective-permute-done.refs_1_
  440.7 0.0 collective-permute-start.6
  440.7 0.5 collective-permute-start.7
  441.2 0.0 collective-permute-done.4.refs_3_
  441.2 0.0 collective-permute-done.5.refs_4_
  441.2 6.3 %shard_map.188 = (f32[8,472,1408]{2,1,0:T(8,128)}, f32[8,472,1408]{2,1,0:T(8,128)S(1)}) custom-call(f32[8,472,1408]{2,1,0:T(8,128)S(1)} %early_out.1.refs_0_, f32[120,1408]{1,0:T(8,128)} %collective-permute-done.2.refs_1_, f32[120,1408]{1,0:T(8,128)} %collective-permute-done.3.refs_2_, ...), custom_call_target="tpu_custom_call", output_to_operand_aliasing={{1}: (0, {})} | custom-call | flops 5316608000 | bytes 42532864 | tf_op jit(solution)/shard_map/pallas_call | solution.py:766
  447.5 0.0 collective-permute-done.7.refs_4_
  447.5 0.0 collective-permute-done.6.refs_3_
  447.5 6.2 %shard_map.189 = (f32[8,472,1408]{2,1,0:T(8,128)}, f32[8,472,1408]{2,1,0:T(8,128)S(1)}) custom-call(f32[8,472,1408]{2,1,0:T(8,128)S(1)} %get-tuple-element.61.refs_0_, f32[120,1408]{1,0:T(8,128)} %collective-permute-done.refs_1_, f32[112,1408]{1,0:T(8,128)} %collective-permute-done.1.refs_2_, ...), custom_call_target="tpu_custom_call", output_to_operand_aliasing={{1}: (0, {}), {0}: (5, {})} | custom-call | flops 5316608000 | bytes 42532864 | tf_op jit(solution)/shard_map/pallas_call | solution.py:766
Async XLA Ops:
  401.6 39.0 %collective-permute-start.1 = (f32[112,1408]{1,0:T(8,128)}, f32[112,1408]{1,0:T(8,128)}, u32[]{:S(2)}, u32[]{:S(2)}) collective-permute-start(f32[112,1408]{1,0:T(8,128)} %get-tuple-element.57.refs_4_), channel_id=1, source_target_pairs={{0,2},{1,3},{2,0},{3,1},{4,6},{5,7},{6,4},{7,5},{8,10},{9,11},{10,... | collective-permute-start | bytes 1892360 | tf_op jit(solution)/shard_map/ppermute | solution.py:830
  402.2 38.4 %collective-permute-start = (f32[120,1408]{1,0:T(8,128)}, f32[120,1408]{1,0:T(8,128)}, u32[]{:S(2)}, u32[]{:S(2)}) collective-permute-start(f32[120,1408]{1,0:T(8,128)} %get-tuple-element.55.refs_2_), channel_id=1, source_target_pairs={{0,4},{1,5},{2,6},{3,7},{4,0},{5,1},{6,2},{7,3},{8,12},{9,13},{10,... | collective-permute-start | bytes 2027528 | tf_op jit(solution)/shard_map/ppermute | solution.py:830
  403.7 30.8 %collective-permute-start.2 = (f32[120,1408]{1,0:T(8,128)}, f32[120,1408]{1,0:T(8,128)}, u32[]{:S(2)}, u32[]{:S(2)}) collective-permute-start(f32[120,1408]{1,0:T(8,128)} %get-tuple-element.54.refs_1_), channel_id=1, source_target_pairs={{0,4},{1,5},{2,6},{3,7},{4,0},{5,1},{6,2},{7,3},{8,12},{9,13},{10,... | collective-permute-start | bytes 2027528 | tf_op jit(solution)/shard_map/ppermute | solution.py:830
  404.2 30.3 %collective-permute-start.3 = (f32[120,1408]{1,0:T(8,128)}, f32[120,1408]{1,0:T(8,128)}, u32[]{:S(2)}, u32[]{:S(2)}) collective-permute-start(f32[120,1408]{1,0:T(8,128)} %get-tuple-element.56.refs_3_), channel_id=1, source_target_pairs={{0,2},{1,3},{2,0},{3,1},{4,6},{5,7},{6,4},{7,5},{8,10},{9,11},{10,... | collective-permute-start | bytes 2027528 | tf_op jit(solution)/shard_map/ppermute | solution.py:830
  434.5 6.7 %collective-permute-start.4 = (f32[120,1408]{1,0:T(8,128)}, f32[120,1408]{1,0:T(8,128)}, u32[]{:S(2)}, u32[]{:S(2)}) collective-permute-start(f32[120,1408]{1,0:T(8,128)} %collective-permute-done.2.refs_1_), channel_id=1, source_target_pairs={{0,1},{1,0},{2,3},{3,2},{4,5},{5,4},{6,7},{7,6},{8,9},{9,8},{10,11... | collective-permute-start | bytes 2027528 | tf_op jit(solution)/shard_map/ppermute | solution.py:830
  434.5 6.7 %collective-permute-start.5 = (f32[120,1408]{1,0:T(8,128)}, f32[120,1408]{1,0:T(8,128)}, u32[]{:S(2)}, u32[]{:S(2)}) collective-permute-start(f32[120,1408]{1,0:T(8,128)} %collective-permute-done.3.refs_2_), channel_id=1, source_target_pairs={{0,1},{1,0},{2,3},{3,2},{4,5},{5,4},{6,7},{7,6},{8,9},{9,8},{10,11... | collective-permute-start | bytes 2027528 | tf_op jit(solution)/shard_map/ppermute | solution.py:830
  440.7 6.8 %collective-permute-start.6 = (f32[120,1408]{1,0:T(8,128)}, f32[120,1408]{1,0:T(8,128)}, u32[]{:S(2)}, u32[]{:S(2)}) collective-permute-start(f32[120,1408]{1,0:T(8,128)} %collective-permute-done.refs_1_), channel_id=1, source_target_pairs={{0,1},{1,0},{2,3},{3,2},{4,5},{5,4},{6,7},{7,6},{8,9},{9,8},{10,11... | collective-permute-start | bytes 2027528 | tf_op jit(solution)/shard_map/ppermute | solution.py:830
  440.7 6.8 %collective-permute-start.7 = (f32[112,1408]{1,0:T(8,128)}, f32[112,1408]{1,0:T(8,128)}, u32[]{:S(2)}, u32[]{:S(2)}) collective-permute-start(f32[112,1408]{1,0:T(8,128)} %collective-permute-done.1.refs_2_), channel_id=1, source_target_pairs={{0,1},{1,0},{2,3},{3,2},{4,5},{5,4},{6,7},{7,6},{8,9},{9,8},{10,11... | collective-permute-start | bytes 1892360 | tf_op jit(solution)/shard_map/ppermute | solution.py:830
